TPU v7x, 32 devices: a whole 2x2x4 slice. The times are simulated.
32 devices in a mesh: cls: 4 (over y, x), dom: 8 (over z, core).
Axes of the slice: x: 2, y: 2, z: 4, core: 2. Of those that a mesh axis runs over, the one named last changes fastest.
Arguments:
- particles: bfloat16 [256, 2, 110592], P(('cls', 'dom')), may hold values from -18 to 18
- labels: int32 [256, 1], P(('cls', 'dom')), may hold values from 0 to 7; in each aligned block of 8 rows (0 to 7, 8 to 15, ...) at most 2 rows name the same one
- wedge_index: int32 [256], P(('cls', 'dom')), may hold values from 0 to 11
- wedge_table: float32 [12, 110592], replicated, may hold values from 0.05 to 1
Outputs:
- class_average: float32 [8, 2, 110592], P('cls', None, 'dom')
- weight_total: float32 [8, 110592], P('cls', 'dom')
Inputs may be any that keep to these rules, and one draw needn't show every extreme that they name: `labels`: among the rows of one device no class appears more than 2 times, and on some devices one class appears exactly 2 times; every class appears on some device.
All inputs are finite; a program needn't handle non-finite values.
Results may differ from a plain program's by a relative error of at most 0.0003.
Values may be sent and summed in bfloat16 or wider, within the bound.
A program may use at most 128 MiB of HBM per device.

v0:
```python
import functools

import jax
import jax.numpy as jnp
from jax import lax
from jax.experimental import pallas as pl
from jax.experimental.pallas import tpu as pltpu
from jax.sharding import PartitionSpec as P

MESH = pl.DeviceIdType.MESH
LANES = 128
LEVELS = 32767.0
CLASSES_PER_GROUP = 2


def divisor(number, cap):
    return max(size for size in range(1, cap + 1) if number % size == 0)


def split2(value):
    high = value.astype(jnp.bfloat16)
    low = (value - high.astype(jnp.float32)).astype(jnp.bfloat16)
    return high, low


def stack2(value):
    high = value.astype(jnp.bfloat16).astype(jnp.float32)
    return jnp.concatenate([high, value - high], axis=0).astype(jnp.bfloat16)


def dot(left, right):
    return jnp.dot(left, right, preferred_element_type=jnp.float32)


def spans_of(start, tiles, cap):
    unit = divisor(tiles, cap)

    def span(index, base=start):
        return pl.ds(pl.multiple_of(base + index * (unit * LANES), LANES), unit * LANES)

    return tiles // unit, unit, span


def encode(read, tiles, start, code_ref, scale_ref):
    turns, unit, span = spans_of(0, tiles, 9)

    def largest(index, top):
        block = jnp.abs(read(span(index, start)))
        for k in range(unit):
            top = jnp.maximum(top, block[:, k * LANES : (k + 1) * LANES])
        return top

    rows = code_ref.shape[0]
    top = lax.fori_loop(0, turns, largest, jnp.zeros((rows, LANES), jnp.float32))
    top = jnp.maximum(top, 1e-30)
    scale_ref[...] = top * (1.0 / LEVELS)
    factor = jnp.concatenate([LEVELS / top] * unit, axis=1)

    def store(index, carry):
        block = read(span(index, start)) * factor
        code_ref[:, span(index)] = jnp.round(block).astype(jnp.int32).astype(jnp.int16)
        return carry

    lax.fori_loop(0, turns, store, 0)


def decoder(code_ref, scale_ref, start, tiles):
    unit = divisor(tiles, 9)
    scale = jnp.concatenate([scale_ref[...]] * unit, axis=1)

    def read(span):
        here = pl.ds(pl.multiple_of(span.start - start, LANES), span.size)
        return code_ref[:, here].astype(jnp.int32).astype(jnp.float32) * scale

    return read


def kernel(
    n_z, shard, p_dev, group_rows, wedges, cuts,
    labels_ref, wedge_ref, x_ref, table_ref, mean_ref, total_ref,
    x_all, aux_own, aux_peer, table, sums, last, tallies,
    load_sem, table_sem, pair_send, pair_recv, aux_send, aux_recv,
    *parts_refs,
):
    cls = lax.axis_index("cls")
    dom = lax.axis_index("dom")
    z = dom // 2
    core = lax.rem(dom, 2)
    peer = dom + 1 - 2 * core
    near = cls + 1 - 2 * lax.rem(cls, 2)
    far = cls + 2 - 4 * (cls // 2)
    both = near + 2 - 4 * (cls // 2)
    n_groups = sums.shape[1]
    rows = 2 * p_dev
    each = len(parts_refs) // len(cuts)
    bufs = [parts_refs[i * each : (i + 1) * each] for i in range(len(cuts))]

    def place(step):
        return lax.rem(z + 1 + step, n_z)

    loads = []
    for step in range(n_z):
        here = place(step) * 2 + core
        span = pl.ds(pl.multiple_of(here * shard, LANES), shard)
        copies = [pltpu.make_async_copy(table_ref.at[:, span], table.at[step], table_sem.at[step])]
        for p in range(p_dev):
            copies.append(
                pltpu.make_async_copy(
                    x_ref.at[p, :, span], x_all.at[step, pl.ds(2 * p, 2)], load_sem.at[step, p]
                )
            )
        for copy in copies:
            copy.start()
        loads.append(copies)

    barrier = pltpu.get_barrier_semaphore()
    pl.semaphore_signal(barrier, inc=1, device_id={"dom": peer}, device_id_type=MESH)
    pl.semaphore_signal(barrier, inc=1, device_id={"cls": near}, device_id_type=MESH)
    pl.semaphore_signal(barrier, inc=1, device_id={"cls": far}, device_id_type=MESH)
    for step in range(n_z - 1):
        pl.semaphore_signal(
            barrier, inc=1, device_id={"dom": place(step) * 2 + core}, device_id_type=MESH
        )

    row = lax.broadcasted_iota(jnp.int32, (rows, LANES), 0)
    lane = lax.broadcasted_iota(jnp.int32, (rows, LANES), 1)
    out_row = lax.broadcasted_iota(jnp.int32, (n_groups * group_rows, LANES), 0)
    out_lane = lax.broadcasted_iota(jnp.int32, (n_groups * group_rows, LANES), 1)
    wedge_of = jnp.zeros((rows, LANES), jnp.int32)
    label_of = jnp.zeros_like(out_row) - 1
    for p in range(p_dev):
        wedge_of = jnp.where((row == 2 * p) | (row == 2 * p + 1), wedge_ref[p], wedge_of)
        label_of = jnp.where(
            (out_lane == 2 * p) | (out_lane == 2 * p + 1), labels_ref[p], label_of
        )
    aux_own[0] = (wedge_of == lane).astype(jnp.float32)
    aux_own[1] = (
        (out_row == 2 * label_of + (out_lane & 1)) & (label_of >= 0)
    ).astype(jnp.float32)

    pl.semaphore_wait(barrier, n_z + 2)

    pair = []
    for step in range(n_z):
        there = place(step) * 2 + (1 - core)
        span = pl.ds(pl.multiple_of(there * shard, LANES), shard)
        copies = []
        for p in range(p_dev):
            copy = pltpu.make_async_remote_copy(
                src_ref=x_ref.at[p, :, span], dst_ref=x_all.at[step, pl.ds(rows + 2 * p, 2)],
                send_sem=pair_send.at[step, p], recv_sem=pair_recv.at[step, p],
                device_id={"dom": peer}, device_id_type=MESH,
            )
            copy.start()
            copies.append(copy)
        pair.append(copies)
    aux_copy = pltpu.make_async_remote_copy(
        src_ref=aux_own, dst_ref=aux_peer, send_sem=aux_send, recv_sem=aux_recv,
        device_id={"dom": peer}, device_id_type=MESH,
    )
    aux_copy.start()
    aux_copy.wait()

    pick_own = aux_own[0].astype(jnp.bfloat16)
    pick_peer = aux_peer[0].astype(jnp.bfloat16)
    member_own = aux_own[1][:, :rows].astype(jnp.bfloat16)
    member_peer = aux_peer[1][:, :rows].astype(jnp.bfloat16)
    counts = dot(member_own, pick_own) + dot(member_peer, pick_peer)
    for group in range(n_groups):
        tallies[group] = counts[group * group_rows : (group + 1) * group_rows]
    pick = jnp.concatenate([aux_own[0], aux_peer[0]], axis=0)[:, :wedges]
    pick = jnp.concatenate([pick, pick], axis=1).astype(jnp.bfloat16)
    member = jnp.concatenate([aux_own[1][:, :rows], aux_peer[1][:, :rows]] * 2, axis=1)
    member = member.astype(jnp.bfloat16)

    def send(source, target, sems, slot, who):
        copy = pltpu.make_async_remote_copy(
            src_ref=source, dst_ref=target, send_sem=sems[0].at[slot], recv_sem=sems[1].at[slot],
            device_id=who, device_id_type=MESH,
        )
        copy.start()
        return copy

    first, second, third = {}, {}, {}

    def compute(step, part):
        start, tiles = cuts[part]
        (q1, c1, r1, d1, q2, c2, r2, d2, q3, c3, r3, d3, sa, sb, ra, rb) = bufs[part]
        if part == 0:
            for copy in loads[step] + pair[step]:
                copy.wait()
        turns, unit, span_of = spans_of(start, tiles, 12)

        @pl.loop(0, turns)
        def _(index):
            span = span_of(index)
            weight = dot(pick, stack2(table[step, :, span]))
            high, low = split2(weight * x_all[step, :, span].astype(jnp.float32))
            total = dot(member, jnp.concatenate([high, low], axis=0))
            for group in range(n_groups):
                sums[step, group, :, span] = total[group * group_rows : (group + 1) * group_rows]

        partner = near if part == 0 else far
        copies = []
        for slot, group in ((1, both), (0, partner)):
            encode(
                lambda span: sums[step, group, :, span], tiles, start,
                q1.at[step, slot], c1.at[step, slot, :, pl.ds(0, LANES)],
            )
            if part == 0:
                c1[step, slot, :, pl.ds(LANES, LANES)] = tallies[group]
            for kind, source, target in ((0, c1, d1), (1, q1, r1)):
                copies.append(
                    send(
                        source.at[step, slot], target.at[step, slot], (sa, ra),
                        4 * step + 2 * slot + kind, {"cls": partner},
                    )
                )
        first[step, part] = copies

    def forward(step, part):
        start, tiles = cuts[part]
        (q1, c1, r1, d1, q2, c2, r2, d2, q3, c3, r3, d3, sa, sb, ra, rb) = bufs[part]
        other = far if part == 0 else near
        for copy in first[step, part][:2]:
            copy.wait()
        got = decoder(r1.at[step, 1], d1.at[step, 1, :, pl.ds(0, LANES)], start, tiles)
        encode(
            lambda span: sums[step, other, :, span] + got(span), tiles, start,
            q2.at[step], c2.at[step, :, pl.ds(0, LANES)],
        )
        if part == 0:
            c2[step, :, pl.ds(LANES, LANES)] = tallies[other] + d1[step, 1, :, pl.ds(LANES, LANES)]
        second[step, part] = [
            send(source.at[step], target.at[step], (sb, rb), 4 * step + kind, {"cls": other})
            for kind, source, target in ((0, c2, d2), (1, q2, r2))
        ]

    def settle(step, part):
        start, tiles = cuts[part]
        (q1, c1, r1, d1, q2, c2, r2, d2, q3, c3, r3, d3, sa, sb, ra, rb) = bufs[part]
        for copy in first[step, part][2:] + second[step, part]:
            copy.wait()
        got1 = decoder(r1.at[step, 0], d1.at[step, 0, :, pl.ds(0, LANES)], start, tiles)
        got2 = decoder(r2.at[step], d2.at[step, :, pl.ds(0, LANES)], start, tiles)

        def read(span):
            return sums[step, cls, :, span] + got1(span) + got2(span)

        tally = None
        if part == 0:
            tally = (
                tallies[cls]
                + d1[step, 0, :, pl.ds(LANES, LANES)]
                + d2[step, :, pl.ds(LANES, LANES)]
            )
        if step == n_z - 1:
            turns, _, span_of = spans_of(start, tiles, 9)

            @pl.loop(0, turns)
            def _(index):
                span = span_of(index)
                last[:, span] = read(span)

            return tally
        encode(read, tiles, start, q3.at[step], c3.at[step, :, pl.ds(0, LANES)])
        if part == 0:
            c3[step, :, pl.ds(LANES, LANES)] = tally
        there = place(step) * 2 + core
        third[step, part] = [
            send(source.at[step], target.at[step], (sb, rb), 4 * step + 2 + kind, {"dom": there})
            for kind, source, target in ((0, c3, d3), (1, q3, r3))
        ]
        return None

    n_parts = len(cuts)
    units = [(step, part) for step in range(n_z) for part in range(n_parts)]
    tally = None
    for turn in range(len(units) + 4):
        if turn < len(units):
            compute(*units[turn])
        if 2 <= turn < len(units) + 2:
            forward(*units[turn - 2])
        if 4 <= turn:
            found = settle(*units[turn - 4])
            tally = found if found is not None else tally

    for part in range(n_parts):
        start, tiles = cuts[part]
        (q1, c1, r1, d1, q2, c2, r2, d2, q3, c3, r3, d3, sa, sb, ra, rb) = bufs[part]
        for step in range(n_z - 1):
            for copy in third[step, part]:
                copy.wait()
        if part == 0:
            for step in range(n_z - 1):
                tally = tally + d3[step, :, pl.ds(LANES, LANES)]
            tally = stack2(tally[:, :wedges])
            tally = jnp.concatenate([tally, tally], axis=1)
        got = [
            decoder(r3.at[step], d3.at[step, :, pl.ds(0, LANES)], start, tiles)
            for step in range(n_z - 1)
        ]
        turns, _, span_of = spans_of(start, tiles, 9)

        @pl.loop(0, turns)
        def _(index):
            span = span_of(index)
            value = last[:, span]
            for read in got:
                value = value + read(span)
            weight = table[n_z - 1, :, span]
            total = dot(tally, stack2(weight * weight))
            total = total[:group_rows] + total[group_rows:]
            mean_ref[:, span] = value / (total + 1.0)
            total_ref[:, span] = total


def finish(mean_ref, total_ref, avg_out, total_out):
    for index in range(avg_out.shape[0]):
        avg_out[index] = mean_ref[pl.ds(2 * index, 2)]
        total_out[pl.ds(index, 1)] = total_ref[pl.ds(2 * index, 1)]


def per_device(classes, particles, labels, wedge_index, wedge_table):
    n_cls = lax.axis_size("cls")
    n_dom = lax.axis_size("dom")
    p_dev, _, voxels = particles.shape
    wedges = wedge_table.shape[0]
    shard = voxels // n_dom
    n_z = n_dom // 2
    group = classes // n_cls
    rows = 2 * p_dev
    out_rows = 2 * group
    tiles = shard // LANES
    cuts = ((0, tiles // 2), (tiles // 2 * LANES, tiles - tiles // 2))
    any_space = pl.BlockSpec(memory_space=pl.ANY)
    vmem = pl.BlockSpec(memory_space=pltpu.VMEM)
    smem = pl.BlockSpec(memory_space=pltpu.SMEM)
    dma = pltpu.SemaphoreType.DMA
    scratch = [
        pltpu.VMEM((n_z, 2 * rows, shard), jnp.bfloat16),
        pltpu.VMEM((2, rows, LANES), jnp.float32),
        pltpu.VMEM((2, rows, LANES), jnp.float32),
        pltpu.VMEM((n_z, wedges, shard), jnp.float32),
        pltpu.VMEM((n_z, n_cls, out_rows, shard), jnp.float32),
        pltpu.VMEM((out_rows, shard), jnp.float32),
        pltpu.VMEM((n_cls, out_rows, LANES), jnp.float32),
        dma((n_z, p_dev)), dma((n_z,)), dma((n_z, p_dev)), dma((n_z, p_dev)), dma, dma,
    ]
    for part, (_, count) in enumerate(cuts):
        wide = LANES * (2 if part == 0 else 1)
        for lead in ((n_z, 2), (n_z,), (n_z,)):
            for _ in range(2):
                scratch.append(pltpu.VMEM((*lead, out_rows, count * LANES), jnp.int16))
                scratch.append(pltpu.VMEM((*lead, out_rows, wide), jnp.float32))
        scratch += [dma((4 * n_z,)) for _ in range(4)]
    mean, total = pl.pallas_call(
        functools.partial(kernel, n_z, shard, p_dev, out_rows, wedges, cuts),
        out_shape=(
            jax.ShapeDtypeStruct((out_rows, shard), jnp.float32),
            jax.ShapeDtypeStruct((out_rows, shard), jnp.float32),
        ),
        in_specs=[smem, smem, any_space, any_space],
        out_specs=(vmem, vmem),
        scratch_shapes=scratch,
        compiler_params=pltpu.CompilerParams(
            collective_id=0, has_side_effects=True, vmem_limit_bytes=60 * 1024 * 1024
        ),
    )(labels.reshape(p_dev), wedge_index, particles, wedge_table)
    return pl.pallas_call(
        finish,
        out_shape=(
            jax.ShapeDtypeStruct((group, 2, shard), jnp.float32),
            jax.ShapeDtypeStruct((group, shard), jnp.float32),
        ),
        in_specs=[vmem, vmem],
        out_specs=(vmem, vmem),
    )(mean, total)


def solution(mesh):
    classes = CLASSES_PER_GROUP * mesh.shape["cls"]
    return jax.shard_map(
        functools.partial(per_device, classes),
        mesh=mesh,
        in_specs=(P(("cls", "dom"), None, None), P(("cls", "dom"), None), P(("cls", "dom")), P()),
        out_specs=(P("cls", None, "dom"), P("cls", "dom")),
        check_vma=False,
    )
```

profile of v0, /device:TPU:0, one launch (start us, length us, event | category | flops | bytes accessed | tf_op | source)
XLA Modules:
  0.0 42.8 jit_solution(13380843717155602836)
XLA Ops:
  0.6 40.3 %shard_map.59 = (f32[4,13824]{1,0:T(4,128)}, f32[4,13824]{1,0:T(4,128)}) custom-call(s32[8]{0:T(128)} %bitcast.1, s32[8]{0:T(128)} %wedge_ref.1, bf16[8,2,110592]{2,1,0:T(2,128)(2,1)} %x_ref.1, f32[12,110592]{1,0:T(8,128)} %table_ref.1), custom_call_target="tpu_custom_call" | custom-call | tf_op jit(solution)/shard_map/pallas_call | solution.py:357
  41.0 1.8 %shard_map.60 = (f32[2,2,13824]{2,1,0:T(2,128)}, f32[2,13824]{1,0:T(2,128)}) custom-call(f32[4,13824]{1,0:T(4,128)} %get-tuple-element.4.mean_ref, f32[4,13824]{1,0:T(4,128)} %get-tuple-element.5.total_ref), custom_call_target="tpu_custom_call" | custom-call | tf_op jit(solution)/shard_map/pallas_call | solution.py:370
where the time goes:
time: 43 us; the launch traced here: 42.8 us
  Pallas kernels  42.1 us (98%)
  between operations  0.64 us (1%)
    pallas_call x1, Pallas kernels, per_device(): pl.pallas_call(functools.partial(kernel, n_z, shard, p_dev, out_rows, wed...  40.3 us
    pallas_call x1, Pallas kernels, per_device(): pl.pallas_call(finish, out_shape=(jax.ShapeDtypeStruct((group, 2, shard),...  1.8 us

commit v1 on v0

v1 whole, which is shorter than its diff:
```python
import functools

import jax
import jax.numpy as jnp
from jax import lax
from jax.experimental import pallas as pl
from jax.experimental.pallas import tpu as pltpu
from jax.sharding import PartitionSpec as P

MESH = pl.DeviceIdType.MESH
LANES = 128
LEVELS = 32767.0
CLASSES_PER_GROUP = 2
GROUP_ROWS = 2 * CLASSES_PER_GROUP
PAIR_ROWS = 2 * GROUP_ROWS
PICK_TILES = 36
SUM_TILES = 27
CODE_TILES = 27
FORWARD_LAG = 2
SETTLE_LAG = 4


def divisor(number, cap):
    return max(size for size in range(1, cap + 1) if number % size == 0)


def dot(left, right):
    return jnp.dot(left, right, preferred_element_type=jnp.float32)


def stack2(value):
    high = value.astype(jnp.bfloat16)
    low = (value - high.astype(jnp.float32)).astype(jnp.bfloat16)
    return jnp.concatenate([high, low], axis=0)


def stack2_rows(value):
    high = value.astype(jnp.bfloat16).astype(jnp.float32)
    return jnp.concatenate([high, value - high], axis=0).astype(jnp.bfloat16)


def walk(start, tiles, cap, body):
    unit = divisor(tiles, cap)
    turns = tiles // unit
    if turns == 1:
        body(pl.ds(start, unit * LANES), unit)
        return

    @pl.loop(0, turns)
    def _(index):
        body(pl.ds(pl.multiple_of(start + index * (unit * LANES), LANES), unit * LANES), unit)


def wide(value, unit):
    return jnp.concatenate([value] * unit, axis=1) if unit > 1 else value


def to_code(value):
    return jnp.round(value).astype(jnp.int32).astype(jnp.int16)


def from_code(code):
    return code.astype(jnp.int32).astype(jnp.float32)


def plan_units(n_z, tiles):
    half = tiles // 2
    plain = ((0, half, 0), (half, tiles - half, 1))
    units = []
    for step in range(n_z):
        for part, (start, count, kind) in enumerate(plain):
            units.append((step, part, start * LANES, count, kind))
    return units


def kernel(
    n_z, shard, p_dev, wedges, units,
    labels_ref, wedge_ref, x_ref, table_ref, mean_ref, total_ref,
    label_s, wedge_s, aux_own, aux_peer, x_all, table, weights, sums, inverse, tops,
    q1, r1, c1, d1, q2, r2, c2, d2, q3, r3, c3, d3,
    t1, u1, t2, u2, t3, u3,
    small_sem, load_sem, table_sem, pair_send, pair_recv, aux_send, aux_recv,
    s1, g1, s2, g2, s3, g3, ts, tg,
):
    cls = lax.axis_index("cls")
    dom = lax.axis_index("dom")
    z = dom // 2
    core = lax.rem(dom, 2)
    peer = dom + 1 - 2 * core
    near = cls + 1 - 2 * lax.rem(cls, 2)
    far = cls + 2 - 4 * (cls // 2)
    both = near + 2 - 4 * (cls // 2)
    rows = 2 * p_dev
    tiles = shard // LANES
    last = n_z - 1
    offsets = sorted(range(1, n_z), key=lambda gap: -min(gap, n_z - gap)) + [0]

    def place(step):
        return lax.rem(z + offsets[step], n_z)

    small = [
        pltpu.make_async_copy(labels_ref, label_s, small_sem.at[0]),
        pltpu.make_async_copy(wedge_ref, wedge_s, small_sem.at[1]),
    ]
    for copy in small:
        copy.start()

    barrier = pltpu.get_barrier_semaphore()
    pl.semaphore_signal(barrier, inc=1, device_id={"dom": peer}, device_id_type=MESH)
    pl.semaphore_signal(barrier, inc=1, device_id={"cls": near}, device_id_type=MESH)
    pl.semaphore_signal(barrier, inc=1, device_id={"cls": far}, device_id_type=MESH)
    for step in range(last):
        pl.semaphore_signal(
            barrier, inc=1, device_id={"dom": place(step) * 2 + core}, device_id_type=MESH
        )

    loads, tables = [], []
    for step in range(n_z):
        here = place(step) * 2 + core
        span = pl.ds(pl.multiple_of(here * shard, LANES), shard)
        copy = pltpu.make_async_copy(table_ref.at[:, span], table.at[step], table_sem.at[step])
        copy.start()
        tables.append(copy)
        copies = []
        for p in range(p_dev):
            copy = pltpu.make_async_copy(
                x_ref.at[p, :, span], x_all.at[step, pl.ds(2 * p, 2)], load_sem.at[step, p]
            )
            copy.start()
            copies.append(copy)
        loads.append(copies)

    for copy in small:
        copy.wait()
    row = lax.broadcasted_iota(jnp.int32, (rows, LANES), 0)
    lane = lax.broadcasted_iota(jnp.int32, (rows, LANES), 1)
    out_row = lax.broadcasted_iota(jnp.int32, (4 * GROUP_ROWS, LANES), 0)
    out_lane = lax.broadcasted_iota(jnp.int32, (4 * GROUP_ROWS, LANES), 1)
    wedge_of = jnp.zeros((rows, LANES), jnp.int32)
    label_of = jnp.zeros_like(out_row)
    particle = (out_lane & (rows - 1)) // 2
    for p in range(p_dev):
        wedge_of = jnp.where(row // 2 == p, wedge_s[p], wedge_of)
        label_of = jnp.where(particle == p, label_s[p], label_of)
    column = jnp.where(lane >= wedges, lane - wedges, lane)
    aux_own[0] = ((wedge_of == column) & (lane < 2 * wedges)).astype(jnp.float32)
    within = (out_row // 2) % CLASSES_PER_GROUP
    place_of = out_row // GROUP_ROWS
    for kind, order in enumerate(((cls, far, near, both), (cls, near, far, both))):
        target = jnp.zeros_like(out_row)
        for slot, group in enumerate(order):
            target = jnp.where(place_of == slot, CLASSES_PER_GROUP * group + within, target)
        aux_own[1 + kind] = (
            (target == label_of) & ((out_row & 1) == (out_lane & 1))
        ).astype(jnp.float32)

    pl.semaphore_wait(barrier, n_z + 2)

    aux_copy = pltpu.make_async_remote_copy(
        src_ref=aux_own, dst_ref=aux_peer, send_sem=aux_send, recv_sem=aux_recv,
        device_id={"dom": peer}, device_id_type=MESH,
    )
    aux_copy.start()
    pair = []
    for step in range(n_z):
        there = place(step) * 2 + (1 - core)
        span = pl.ds(pl.multiple_of(there * shard, LANES), shard)
        copies = []
        for p in range(p_dev):
            copy = pltpu.make_async_remote_copy(
                src_ref=x_ref.at[p, :, span], dst_ref=x_all.at[step, pl.ds(rows + 2 * p, 2)],
                send_sem=pair_send.at[step, p], recv_sem=pair_recv.at[step, p],
                device_id={"dom": peer}, device_id_type=MESH,
            )
            copy.start()
            copies.append(copy)
        pair.append(copies)
    aux_copy.wait()

    own_side = (out_lane & rows) == 0
    members = [
        jnp.where(own_side, aux_own[1 + kind], aux_peer[1 + kind])[:, : 4 * rows].astype(jnp.bfloat16)
        for kind in range(2)
    ]
    pick = jnp.concatenate([aux_own[0], aux_peer[0]], axis=0).astype(jnp.bfloat16)
    counts = dot(members[0][:, : 2 * rows], pick)
    pick = pick[:, : 2 * wedges]

    def send(source, target, sems, who):
        copy = pltpu.make_async_remote_copy(
            src_ref=source, dst_ref=target, send_sem=sems[0], recv_sem=sems[1],
            device_id=who, device_id_type=MESH,
        )
        copy.start()
        return copy

    t1[...] = counts[PAIR_ROWS:]
    tally_copies = [send(t1, u1, (ts.at[0], tg.at[0]), {"cls": near})]

    for step in range(n_z):
        tables[step].wait()

        def pick_body(span, unit):
            weights[step, :, span] = dot(pick, stack2_rows(table[step, :, span]))

        walk(0, tiles, PICK_TILES, pick_body)

    first, second, third = {}, {}, {}

    def compute(index):
        step, part, start, count, kind = units[index]
        if start == 0:
            for copy in loads[step] + pair[step]:
                copy.wait()
        member = members[kind]
        tops[index] = jnp.zeros((4 * GROUP_ROWS, LANES), jnp.float32)

        def body(span, unit):
            product = weights[step, :, span] * x_all[step, :, span].astype(jnp.float32)
            total = dot(member, stack2(product))
            sums[step, :, span] = total
            size = jnp.abs(total)
            pieces = [size[:, k * LANES : (k + 1) * LANES] for k in range(unit)]
            while len(pieces) > 1:
                pieces = [
                    jnp.maximum(*pieces[k : k + 2]) if k + 1 < len(pieces) else pieces[k]
                    for k in range(0, len(pieces), 2)
                ]
            tops[index] = jnp.maximum(tops[index], pieces[0])

        walk(start, count, SUM_TILES, body)
        top = jnp.maximum(tops[index, pl.ds(PAIR_ROWS, PAIR_ROWS)], 1e-30)
        c1[index] = top
        factor = LEVELS / top

        def code_body(span, unit):
            q1[step, :, span] = to_code(
                sums[step, pl.ds(PAIR_ROWS, PAIR_ROWS), span] * wide(factor, unit)
            )

        walk(start, count, CODE_TILES, code_body)
        partner = near if kind == 0 else far
        span = pl.ds(start, count * LANES)
        first[index] = [
            send(c1.at[index], d1.at[index], (s1.at[index, 0], g1.at[index, 0]), {"cls": partner}),
            send(q1.at[step, :, span], r1.at[step, :, span], (s1.at[index, 1], g1.at[index, 1]), {"cls": partner}),
        ]

    def forward(index):
        step, part, start, count, kind = units[index]
        for copy in first[index]:
            copy.wait()
        got = d1[index]
        bound = jnp.maximum(tops[index, pl.ds(0, PAIR_ROWS)], 1e-30) + got
        tops[index, pl.ds(0, PAIR_ROWS)] = bound
        scale = got * (1.0 / LEVELS)
        factor = LEVELS / bound
        c2[index] = bound[GROUP_ROWS:]

        def body(span, unit):
            total = sums[step, pl.ds(0, PAIR_ROWS), span] + from_code(r1[step, :, span]) * wide(scale, unit)
            sums[step, pl.ds(0, PAIR_ROWS), span] = total
            q2[step, :, span] = to_code(total * wide(factor, unit))[GROUP_ROWS:]

        walk(start, count, CODE_TILES, body)
        other = far if kind == 0 else near
        span = pl.ds(start, count * LANES)
        second[index] = [
            send(c2.at[index], d2.at[index], (s2.at[index, 0], g2.at[index, 0]), {"cls": other}),
            send(q2.at[step, :, span], r2.at[step, :, span], (s2.at[index, 1], g2.at[index, 1]), {"cls": other}),
        ]

    def settle(index):
        step, part, start, count, kind = units[index]
        for copy in second[index]:
            copy.wait()
        got = d2[index]
        scale = got * (1.0 / LEVELS)
        if step == last:

            def final_body(span, unit):
                value = sums[step, pl.ds(0, GROUP_ROWS), span] + from_code(r2[step, :, span]) * wide(scale, unit)
                mean_ref[:, span] = value * inverse[:, span]

            walk(start, count, CODE_TILES, final_body)
            return
        bound = tops[index, pl.ds(0, GROUP_ROWS)] + got
        c3[index] = bound
        factor = LEVELS / bound

        def body(span, unit):
            value = sums[step, pl.ds(0, GROUP_ROWS), span] + from_code(r2[step, :, span]) * wide(scale, unit)
            q3[step, :, span] = to_code(value * wide(factor, unit))

        walk(start, count, CODE_TILES, body)
        there = {"dom": place(step) * 2 + core}
        span = pl.ds(start, count * LANES)
        third[index] = [
            send(c3.at[index], d3.at[index], (s3.at[index, 0], g3.at[index, 0]), there),
            send(q3.at[step, :, span], r3.at[step, :, span], (s3.at[index, 1], g3.at[index, 1]), there),
        ]

    def gather(index):
        step, part, start, count, kind = units[index]
        mine = [k for k, unit in enumerate(units) if unit[0] < last and unit[1] == part]
        for k in mine:
            for copy in third[k]:
                copy.wait()
        scales = [d3[k] * (1.0 / LEVELS) for k in mine]

        def body(span, unit):
            value = sums[step, pl.ds(0, GROUP_ROWS), span]
            for k, scale in zip(mine, scales):
                value = value + from_code(r3[units[k][0], :, span]) * wide(scale, unit)
            sums[step, pl.ds(0, GROUP_ROWS), span] = value

        walk(start, count, CODE_TILES, body)

    def tally_forward():
        tally_copies[0].wait()
        gathered = counts[:PAIR_ROWS] + u1[...]
        t2[...] = gathered
        tally_copies.append(send(t2, u2, (ts.at[1], tg.at[1]), {"cls": far}))

    def tally_settle():
        tally_copies[1].wait()
        t3[...] = t2[pl.ds(0, GROUP_ROWS)] + u2[pl.ds(GROUP_ROWS, GROUP_ROWS)]
        for step in range(last):
            tally_copies.append(
                send(t3, u3.at[step], (ts.at[2 + step], tg.at[2 + step]), {"dom": place(step) * 2 + core})
            )

    def tally_final():
        tally = t3[...]
        for step in range(last):
            tally_copies[2 + step].wait()
            tally = tally + u3[step]
        tally = stack2_rows(tally[:, : 2 * wedges])

        def body(span, unit):
            weight = table[last, :, span]
            total = dot(tally, stack2_rows(weight * weight))
            total = total[:GROUP_ROWS] + total[GROUP_ROWS:]
            total_ref[:, span] = total
            inverse[:, span] = 1.0 / (total + 1.0)

        walk(0, tiles, SUM_TILES, body)

    n_units = len(units)
    for turn in range(n_units):
        compute(turn)
        if turn == 1:
            tally_forward()
        if turn == 3:
            tally_settle()
        if turn == 5:
            tally_final()
        if turn >= FORWARD_LAG:
            forward(turn - FORWARD_LAG)
        if turn >= SETTLE_LAG:
            settle(turn - SETTLE_LAG)
    lasts = [k for k, unit in enumerate(units) if unit[0] == last]
    pending = [k for k in range(max(0, n_units - SETTLE_LAG), n_units)]
    for k in range(max(0, n_units - FORWARD_LAG), n_units):
        forward(k)
        if pending and pending[0] not in lasts:
            settle(pending.pop(0))
    while pending and pending[0] not in lasts:
        settle(pending.pop(0))
    for k in lasts:
        gather(k)
    for k in pending:
        settle(k)


def finish(mean_ref, total_ref, avg_out, total_out):
    for index in range(avg_out.shape[0]):
        avg_out[index] = mean_ref[pl.ds(2 * index, 2)]
        total_out[pl.ds(index, 1)] = total_ref[pl.ds(2 * index, 1)]


def per_device(particles, labels, wedge_index, wedge_table):
    n_dom = lax.axis_size("dom")
    p_dev, _, voxels = particles.shape
    wedges = wedge_table.shape[0]
    shard = voxels // n_dom
    n_z = n_dom // 2
    rows = 2 * p_dev
    tiles = shard // LANES
    units = plan_units(n_z, tiles)
    count = len(units)
    any_space = pl.BlockSpec(memory_space=pl.ANY)
    vmem = pl.BlockSpec(memory_space=pltpu.VMEM)
    dma = pltpu.SemaphoreType.DMA
    f32 = jnp.float32
    scratch = [
        pltpu.SMEM((p_dev,), jnp.int32),
        pltpu.SMEM((p_dev,), jnp.int32),
        pltpu.VMEM((3, rows, LANES), f32),
        pltpu.VMEM((3, rows, LANES), f32),
        pltpu.VMEM((n_z, 2 * rows, shard), jnp.bfloat16),
        pltpu.VMEM((n_z, wedges, shard), f32),
        pltpu.VMEM((n_z, 2 * rows, shard), f32),
        pltpu.VMEM((n_z, 4 * GROUP_ROWS, shard), f32),
        pltpu.VMEM((GROUP_ROWS, shard), f32),
        pltpu.VMEM((count, 4 * GROUP_ROWS, LANES), f32),
    ]
    for height in (PAIR_ROWS, GROUP_ROWS, GROUP_ROWS):
        scratch += [pltpu.VMEM((n_z, height, shard), jnp.int16)] * 2
        scratch += [pltpu.VMEM((count, height, LANES), f32)] * 2
    scratch += [pltpu.VMEM((PAIR_ROWS, LANES), f32)] * 4
    scratch += [pltpu.VMEM((GROUP_ROWS, LANES), f32), pltpu.VMEM((n_z, GROUP_ROWS, LANES), f32)]
    scratch += [dma((2,)), dma((n_z, p_dev)), dma((n_z,)), dma((n_z, p_dev)), dma((n_z, p_dev)), dma, dma]
    scratch += [dma((count, 2))] * 6
    scratch += [dma((n_z + 1,))] * 2
    mean, total = pl.pallas_call(
        functools.partial(kernel, n_z, shard, p_dev, wedges, units),
        out_shape=(
            jax.ShapeDtypeStruct((GROUP_ROWS, shard), f32),
            jax.ShapeDtypeStruct((GROUP_ROWS, shard), f32),
        ),
        in_specs=[any_space] * 4,
        out_specs=(vmem, vmem),
        scratch_shapes=scratch,
        compiler_params=pltpu.CompilerParams(
            collective_id=0, has_side_effects=True, vmem_limit_bytes=48 * 1024 * 1024
        ),
    )(labels.reshape(p_dev), wedge_index, particles, wedge_table)
    return pl.pallas_call(
        finish,
        out_shape=(
            jax.ShapeDtypeStruct((CLASSES_PER_GROUP, 2, shard), f32),
            jax.ShapeDtypeStruct((CLASSES_PER_GROUP, shard), f32),
        ),
        in_specs=[vmem, vmem],
        out_specs=(vmem, vmem),
    )(mean, total)


def solution(mesh):
    return jax.shard_map(
        per_device,
        mesh=mesh,
        in_specs=(P(("cls", "dom"), None, None), P(("cls", "dom"), None), P(("cls", "dom")), P()),
        out_specs=(P("cls", None, "dom"), P("cls", "dom")),
        check_vma=False,
    )
```

time: 43 us -> 40.5 us (0.942)
  Pallas kernels: 42.1 us -> 35 us
  local copies, waits for them, and re-layouts: 0 us -> 4.64 us
    pallas_call x2, Pallas kernels: 42.1 us -> 35 us  [the longest x1 33.2 us: per_device(): pl.pallas_call(functools.partial(kernel, n_z, shard, p_dev, wedges, units...]
    unnamed x0 -> x10, local copies, waits for them, and re-layouts: none -> 4.64 us
where the time goes in v1:
time: 40.5 us; the launch traced here: 40.3 us
  Pallas kernels  35 us (86%)
  local copies, waits for them, and re-layouts  4.64 us (11%)
  between operations  0.66 us (2%)
    pallas_call x1, Pallas kernels, per_device(): pl.pallas_call(functools.partial(kernel, n_z, shard, p_dev, wedges, units...  33.2 us
    unnamed x10, local copies, waits for them, and re-layouts  4.64 us
    pallas_call x1, Pallas kernels, per_device(): pl.pallas_call(finish, out_shape=(jax.ShapeDtypeStruct((CLASSES_PER_GROUP...  1.8 us

profile of v1, /device:TPU:0, one launch (start us, length us, event | category | flops | bytes accessed | tf_op | source)
XLA Modules:
  0.0 40.3 jit_solution(459690725270813267)
XLA Ops:
  0.6 0.0 copy-start
  0.6 2.0 %copy-done = bf16[8,2,110592]{2,1,0:T(2,128)(2,1)S(1)} copy-done((bf16[8,2,110592]{2,1,0:T(2,128)(2,1)S(1)}, bf16[8,2,110592]{2,1,0:T(2,128)(2,1)}, u32[]{:S(2)}) %copy-start) | copy-done | bytes 3538968
  2.6 0.0 copy-start.3
  2.6 0.7 %copy-done.3 = s32[8,1]{0,1:T(1,128)S(1)} copy-done((s32[8,1]{0,1:T(1,128)S(1)}, s32[8,1]{0,1:T(1,128)}, u32[]{:S(2)}) %copy-start.3) | copy-done | bytes 56
  3.3 0.0 copy-start.4
  3.3 0.7 %copy-done.4 = s32[8]{0:T(128)S(1)} copy-done((s32[8]{0:T(128)S(1)}, s32[8]{0:T(128)}, u32[]{:S(2)}) %copy-start.4) | copy-done | bytes 56
  3.9 33.2 %shard_map.59 = (f32[4,13824]{1,0:T(4,128)S(1)}, f32[4,13824]{1,0:T(4,128)S(1)}) custom-call(s32[8]{0:T(128)S(1)} %bitcast.1, s32[8]{0:T(128)S(1)} %copy-done.4, bf16[8,2,110592]{2,1,0:T(2,128)(2,1)S(1)} %copy-done, f32[12,110592]{1,0:T(8,128)} %table_ref.1), custom_call_target="tpu_custom_call" | custom-call | tf_op jit(solution)/shard_map/pallas_call | solution.py:416
  37.1 0.0 copy-start.1
  37.2 0.7 %copy-done.1 = f32[4,13824]{1,0:T(4,128)} copy-done((f32[4,13824]{1,0:T(4,128)}, f32[4,13824]{1,0:T(4,128)S(1)}, u32[]{:S(2)}) %copy-start.1) | copy-done | bytes 221208
  37.8 0.0 copy-start.2
  37.8 0.7 %copy-done.2 = f32[4,13824]{1,0:T(4,128)} copy-done((f32[4,13824]{1,0:T(4,128)}, f32[4,13824]{1,0:T(4,128)S(1)}, u32[]{:S(2)}) %copy-start.2) | copy-done | bytes 221208
  38.5 1.8 %shard_map.60 = (f32[2,2,13824]{2,1,0:T(2,128)}, f32[2,13824]{1,0:T(2,128)}) custom-call(f32[4,13824]{1,0:T(4,128)} %copy-done.1, f32[4,13824]{1,0:T(4,128)} %copy-done.2), custom_call_target="tpu_custom_call" | custom-call | tf_op jit(solution)/shard_map/pallas_call | solution.py:429
Async XLA Ops:
  0.6 2.0 %copy-start = (bf16[8,2,110592]{2,1,0:T(2,128)(2,1)S(1)}, bf16[8,2,110592]{2,1,0:T(2,128)(2,1)}, u32[]{:S(2)}) copy-start(bf16[8,2,110592]{2,1,0:T(2,128)(2,1)} %x_ref.1) | copy-start | bytes 10616836
  2.6 0.7 %copy-start.3 = (s32[8,1]{0,1:T(1,128)S(1)}, s32[8,1]{0,1:T(1,128)}, u32[]{:S(2)}) copy-start(s32[8,1]{0,1:T(1,128)} %param.5) | copy-start | bytes 100
  3.3 0.7 %copy-start.4 = (s32[8]{0:T(128)S(1)}, s32[8]{0:T(128)}, u32[]{:S(2)}) copy-start(s32[8]{0:T(128)} %wedge_ref.1) | copy-start | bytes 100
  37.1 0.7 %copy-start.1 = (f32[4,13824]{1,0:T(4,128)}, f32[4,13824]{1,0:T(4,128)S(1)}, u32[]{:S(2)}) copy-start(f32[4,13824]{1,0:T(4,128)S(1)} %get-tuple-element.4.mean_ref) | copy-start | bytes 663556
  37.8 0.7 %copy-start.2 = (f32[4,13824]{1,0:T(4,128)}, f32[4,13824]{1,0:T(4,128)S(1)}, u32[]{:S(2)}) copy-start(f32[4,13824]{1,0:T(4,128)S(1)} %get-tuple-element.5.total_ref) | copy-start | bytes 663556

commit v2 on v1

--- a/solution.py
+++ b/solution.py
@@ -10,6 +10,9 @@
 MESH = pl.DeviceIdType.MESH
 LANES = 128
 LEVELS = 32767.0
+SCALE_STEPS = 128.0
+TINY = 1e-30
+HEAD = 2
 CLASSES_PER_GROUP = 2
 GROUP_ROWS = 2 * CLASSES_PER_GROUP
 PAIR_ROWS = 2 * GROUP_ROWS
@@ -63,6 +66,14 @@
     return code.astype(jnp.int32).astype(jnp.float32)
 
 
+def scale_code(bound):
+    return (jnp.ceil(jnp.log2(bound) * SCALE_STEPS) + 1.0).astype(jnp.int32).astype(jnp.int16)
+
+
+def scale_of(code):
+    return jnp.exp2(from_code(code) * (1.0 / SCALE_STEPS))
+
+
 def plan_units(n_z, tiles):
     half = tiles // 2
     plain = ((0, half, 0), (half, tiles - half, 1))
@@ -76,11 +87,10 @@
 def kernel(
     n_z, shard, p_dev, wedges, units,
     labels_ref, wedge_ref, x_ref, table_ref, mean_ref, total_ref,
-    label_s, wedge_s, aux_own, aux_peer, x_all, table, weights, sums, inverse, tops,
-    q1, r1, c1, d1, q2, r2, c2, d2, q3, r3, c3, d3,
-    t1, u1, t2, u2, t3, u3,
+    label_s, wedge_s, aux_own, aux_peer, x_all, table, weights, sums, inverse, tops, tallies,
+    q1, r1, q2, r2, q3, r3, t3, u3,
     small_sem, load_sem, table_sem, pair_send, pair_recv, aux_send, aux_recv,
-    s1, g1, s2, g2, s3, g3, ts, tg,
+    s1, g1, s2, g2, s3, g3, ts, tg, ready,
 ):
     cls = lax.axis_index("cls")
     dom = lax.axis_index("dom")
@@ -106,13 +116,13 @@
         copy.start()
 
     barrier = pltpu.get_barrier_semaphore()
-    pl.semaphore_signal(barrier, inc=1, device_id={"dom": peer}, device_id_type=MESH)
-    pl.semaphore_signal(barrier, inc=1, device_id={"cls": near}, device_id_type=MESH)
-    pl.semaphore_signal(barrier, inc=1, device_id={"cls": far}, device_id_type=MESH)
-    for step in range(last):
-        pl.semaphore_signal(
-            barrier, inc=1, device_id={"dom": place(step) * 2 + core}, device_id_type=MESH
-        )
+
+    def signal(sem, who):
+        pl.semaphore_signal(sem, inc=1, device_id=who, device_id_type=MESH)
+
+    @pl.when(core == 1)
+    def _():
+        signal(barrier, {"dom": peer})
 
     loads, tables = [], []
     for step in range(n_z):
@@ -129,6 +139,19 @@
             copy.start()
             copies.append(copy)
         loads.append(copies)
+
+    @pl.when(core == 0)
+    def _():
+        pl.semaphore_wait(barrier, 1)
+        signal(ready, {"dom": peer})
+
+    @pl.when(core == 1)
+    def _():
+        pl.semaphore_wait(ready, 1)
+        signal(barrier, {"cls": near})
+        signal(barrier, {"cls": far})
+        for step in range(last):
+            signal(barrier, {"dom": place(step) * 2 + core})
 
     for copy in small:
         copy.wait()
@@ -154,8 +177,6 @@
             (target == label_of) & ((out_row & 1) == (out_lane & 1))
         ).astype(jnp.float32)
 
-    pl.semaphore_wait(barrier, n_z + 2)
-
     aux_copy = pltpu.make_async_remote_copy(
         src_ref=aux_own, dst_ref=aux_peer, send_sem=aux_send, recv_sem=aux_recv,
         device_id={"dom": peer}, device_id_type=MESH,
@@ -194,18 +215,28 @@
         copy.start()
         return copy
 
-    t1[...] = counts[PAIR_ROWS:]
-    tally_copies = [send(t1, u1, (ts.at[0], tg.at[0]), {"cls": near})]
-
-    for step in range(n_z):
+    def pick_weights(step):
         tables[step].wait()
 
-        def pick_body(span, unit):
+        def body(span, unit):
             weights[step, :, span] = dot(pick, stack2_rows(table[step, :, span]))
 
-        walk(0, tiles, PICK_TILES, pick_body)
-
-    first, second, third = {}, {}, {}
+        walk(0, tiles, PICK_TILES, body)
+
+    def wire(ref, index, tally=False):
+        step, part, start, count, kind = units[index]
+        begin = start + part * (HEAD * LANES)
+        return ref.at[step, :, pl.ds(begin, (count + 1 + tally) * LANES)]
+
+    def head(index, extra=0):
+        step, part, start, count, kind = units[index]
+        return pl.ds(start + part * (HEAD * LANES) + (count + extra) * LANES, LANES)
+
+    def shifted(span, index):
+        begin = span.start + units[index][1] * (HEAD * LANES)
+        return pl.ds(begin if isinstance(begin, int) else pl.multiple_of(begin, LANES), span.size)
+
+    first, second, third, tally_copies = {}, {}, {}, []
 
     def compute(index):
         step, part, start, count, kind = units[index]
@@ -229,111 +260,118 @@
             tops[index] = jnp.maximum(tops[index], pieces[0])
 
         walk(start, count, SUM_TILES, body)
-        top = jnp.maximum(tops[index, pl.ds(PAIR_ROWS, PAIR_ROWS)], 1e-30)
-        c1[index] = top
-        factor = LEVELS / top
+        code = scale_code(jnp.maximum(tops[index, pl.ds(PAIR_ROWS, PAIR_ROWS)], TINY))
+        q1[step, :, head(index)] = code
+        if index == 0:
+            q1[step, :, head(index, 1)] = to_code(counts[PAIR_ROWS:])
+        factor = LEVELS / scale_of(code)
 
         def code_body(span, unit):
-            q1[step, :, span] = to_code(
+            q1[step, :, shifted(span, index)] = to_code(
                 sums[step, pl.ds(PAIR_ROWS, PAIR_ROWS), span] * wide(factor, unit)
             )
 
         walk(start, count, CODE_TILES, code_body)
+        if index == 0:
+            all_entered()
         partner = near if kind == 0 else far
-        span = pl.ds(start, count * LANES)
-        first[index] = [
-            send(c1.at[index], d1.at[index], (s1.at[index, 0], g1.at[index, 0]), {"cls": partner}),
-            send(q1.at[step, :, span], r1.at[step, :, span], (s1.at[index, 1], g1.at[index, 1]), {"cls": partner}),
-        ]
+        first[index] = send(
+            wire(q1, index, index == 0), wire(r1, index, index == 0),
+            (s1.at[index], g1.at[index]), {"cls": partner},
+        )
+
+    def all_entered():
+        @pl.when(core == 1)
+        def _():
+            pl.semaphore_wait(barrier, n_z + 1)
+            signal(ready, {"dom": peer})
+
+        @pl.when(core == 0)
+        def _():
+            pl.semaphore_wait(ready, 1)
 
     def forward(index):
         step, part, start, count, kind = units[index]
-        for copy in first[index]:
-            copy.wait()
-        got = d1[index]
-        bound = jnp.maximum(tops[index, pl.ds(0, PAIR_ROWS)], 1e-30) + got
+        first[index].wait()
+        got = scale_of(r1[step, :, head(index)])
+        code = scale_code(jnp.maximum(tops[index, pl.ds(0, PAIR_ROWS)], TINY) + got)
+        bound = scale_of(code)
         tops[index, pl.ds(0, PAIR_ROWS)] = bound
+        q2[step, :, head(index)] = code[GROUP_ROWS:]
+        if index == 0:
+            tally = counts[:PAIR_ROWS] + from_code(r1[step, :, head(index, 1)])
+            tallies[...] = tally
+            q2[step, :, head(index, 1)] = to_code(tally)[GROUP_ROWS:]
         scale = got * (1.0 / LEVELS)
         factor = LEVELS / bound
-        c2[index] = bound[GROUP_ROWS:]
-
-        def body(span, unit):
-            total = sums[step, pl.ds(0, PAIR_ROWS), span] + from_code(r1[step, :, span]) * wide(scale, unit)
+
+        def body(span, unit):
+            there = shifted(span, index)
+            total = sums[step, pl.ds(0, PAIR_ROWS), span] + from_code(r1[step, :, there]) * wide(scale, unit)
             sums[step, pl.ds(0, PAIR_ROWS), span] = total
-            q2[step, :, span] = to_code(total * wide(factor, unit))[GROUP_ROWS:]
+            q2[step, :, there] = to_code(total * wide(factor, unit))[GROUP_ROWS:]
 
         walk(start, count, CODE_TILES, body)
         other = far if kind == 0 else near
-        span = pl.ds(start, count * LANES)
-        second[index] = [
-            send(c2.at[index], d2.at[index], (s2.at[index, 0], g2.at[index, 0]), {"cls": other}),
-            send(q2.at[step, :, span], r2.at[step, :, span], (s2.at[index, 1], g2.at[index, 1]), {"cls": other}),
-        ]
+        second[index] = send(
+            wire(q2, index, index == 0), wire(r2, index, index == 0),
+            (s2.at[index], g2.at[index]), {"cls": other},
+        )
 
     def settle(index):
         step, part, start, count, kind = units[index]
-        for copy in second[index]:
-            copy.wait()
-        got = d2[index]
+        second[index].wait()
+        if index == 0:
+            t3[...] = tallies[pl.ds(0, GROUP_ROWS)] + from_code(r2[step, :, head(index, 1)])
+            for other in range(last):
+                tally_copies.append(
+                    send(t3, u3.at[other], (ts.at[other], tg.at[other]), {"dom": place(other) * 2 + core})
+                )
+        got = scale_of(r2[step, :, head(index)])
         scale = got * (1.0 / LEVELS)
         if step == last:
 
             def final_body(span, unit):
-                value = sums[step, pl.ds(0, GROUP_ROWS), span] + from_code(r2[step, :, span]) * wide(scale, unit)
+                there = shifted(span, index)
+                value = sums[step, pl.ds(0, GROUP_ROWS), span] + from_code(r2[step, :, there]) * wide(scale, unit)
                 mean_ref[:, span] = value * inverse[:, span]
 
             walk(start, count, CODE_TILES, final_body)
             return
-        bound = tops[index, pl.ds(0, GROUP_ROWS)] + got
-        c3[index] = bound
-        factor = LEVELS / bound
-
-        def body(span, unit):
-            value = sums[step, pl.ds(0, GROUP_ROWS), span] + from_code(r2[step, :, span]) * wide(scale, unit)
-            q3[step, :, span] = to_code(value * wide(factor, unit))
+        code = scale_code(tops[index, pl.ds(0, GROUP_ROWS)] + got)
+        q3[step, :, head(index)] = code
+        factor = LEVELS / scale_of(code)
+
+        def body(span, unit):
+            there = shifted(span, index)
+            value = sums[step, pl.ds(0, GROUP_ROWS), span] + from_code(r2[step, :, there]) * wide(scale, unit)
+            q3[step, :, there] = to_code(value * wide(factor, unit))
 
         walk(start, count, CODE_TILES, body)
-        there = {"dom": place(step) * 2 + core}
-        span = pl.ds(start, count * LANES)
-        third[index] = [
-            send(c3.at[index], d3.at[index], (s3.at[index, 0], g3.at[index, 0]), there),
-            send(q3.at[step, :, span], r3.at[step, :, span], (s3.at[index, 1], g3.at[index, 1]), there),
-        ]
+        third[index] = send(
+            wire(q3, index), wire(r3, index), (s3.at[index], g3.at[index]),
+            {"dom": place(step) * 2 + core},
+        )
 
     def gather(index):
         step, part, start, count, kind = units[index]
         mine = [k for k, unit in enumerate(units) if unit[0] < last and unit[1] == part]
         for k in mine:
-            for copy in third[k]:
-                copy.wait()
-        scales = [d3[k] * (1.0 / LEVELS) for k in mine]
+            third[k].wait()
+        scales = [scale_of(r3[units[k][0], :, head(k)]) * (1.0 / LEVELS) for k in mine]
 
         def body(span, unit):
             value = sums[step, pl.ds(0, GROUP_ROWS), span]
             for k, scale in zip(mine, scales):
-                value = value + from_code(r3[units[k][0], :, span]) * wide(scale, unit)
+                value = value + from_code(r3[units[k][0], :, shifted(span, k)]) * wide(scale, unit)
             sums[step, pl.ds(0, GROUP_ROWS), span] = value
 
         walk(start, count, CODE_TILES, body)
-
-    def tally_forward():
-        tally_copies[0].wait()
-        gathered = counts[:PAIR_ROWS] + u1[...]
-        t2[...] = gathered
-        tally_copies.append(send(t2, u2, (ts.at[1], tg.at[1]), {"cls": far}))
-
-    def tally_settle():
-        tally_copies[1].wait()
-        t3[...] = t2[pl.ds(0, GROUP_ROWS)] + u2[pl.ds(GROUP_ROWS, GROUP_ROWS)]
-        for step in range(last):
-            tally_copies.append(
-                send(t3, u3.at[step], (ts.at[2 + step], tg.at[2 + step]), {"dom": place(step) * 2 + core})
-            )
 
     def tally_final():
         tally = t3[...]
         for step in range(last):
-            tally_copies[2 + step].wait()
+            tally_copies[step].wait()
             tally = tally + u3[step]
         tally = stack2_rows(tally[:, : 2 * wedges])
 
@@ -347,13 +385,12 @@
         walk(0, tiles, SUM_TILES, body)
 
     n_units = len(units)
+    pick_weights(0)
     for turn in range(n_units):
         compute(turn)
-        if turn == 1:
-            tally_forward()
-        if turn == 3:
-            tally_settle()
-        if turn == 5:
+        if turn + 1 < n_units and units[turn + 1][0] > units[turn][0]:
+            pick_weights(units[turn + 1][0])
+        if turn == 7:
             tally_final()
         if turn >= FORWARD_LAG:
             forward(turn - FORWARD_LAG)
@@ -404,15 +441,15 @@
         pltpu.VMEM((n_z, 4 * GROUP_ROWS, shard), f32),
         pltpu.VMEM((GROUP_ROWS, shard), f32),
         pltpu.VMEM((count, 4 * GROUP_ROWS, LANES), f32),
+        pltpu.VMEM((PAIR_ROWS, LANES), f32),
     ]
+    long = shard + len([unit for unit in units if unit[0] == 0]) * HEAD * LANES
     for height in (PAIR_ROWS, GROUP_ROWS, GROUP_ROWS):
-        scratch += [pltpu.VMEM((n_z, height, shard), jnp.int16)] * 2
-        scratch += [pltpu.VMEM((count, height, LANES), f32)] * 2
-    scratch += [pltpu.VMEM((PAIR_ROWS, LANES), f32)] * 4
+        scratch += [pltpu.VMEM((n_z, height, long), jnp.int16)] * 2
     scratch += [pltpu.VMEM((GROUP_ROWS, LANES), f32), pltpu.VMEM((n_z, GROUP_ROWS, LANES), f32)]
     scratch += [dma((2,)), dma((n_z, p_dev)), dma((n_z,)), dma((n_z, p_dev)), dma((n_z, p_dev)), dma, dma]
-    scratch += [dma((count, 2))] * 6
-    scratch += [dma((n_z + 1,))] * 2
+    scratch += [dma((count,))] * 6
+    scratch += [dma((n_z,))] * 2 + [pltpu.SemaphoreType.REGULAR]
     mean, total = pl.pallas_call(
         functools.partial(kernel, n_z, shard, p_dev, wedges, units),
         out_shape=(
@@ -423,7 +460,7 @@
         out_specs=(vmem, vmem),
         scratch_shapes=scratch,
         compiler_params=pltpu.CompilerParams(
-            collective_id=0, has_side_effects=True, vmem_limit_bytes=48 * 1024 * 1024
+            collective_id=0, has_side_effects=True, vmem_limit_bytes=60 * 1024 * 1024
         ),
     )(labels.reshape(p_dev), wedge_index, particles, wedge_table)
     return pl.pallas_call(

time: 40.5 us -> 32.2 us (0.80)
  local copies, waits for them, and re-layouts: 4.64 us -> 0 us
  Pallas kernels: 35 us -> 31.4 us
    unnamed x10 -> x0, local copies, waits for them, and re-layouts: 4.64 us -> none
    pallas_call x1, Pallas kernels: 33.2 us -> 29.6 us  [per_device(): pl.pallas_call(functools.partial(kernel, n_z, shard, p_dev, wedges, units...]
where the time goes in v2:
time: 32.2 us; the launch traced here: 32 us
  Pallas kernels  31.4 us (98%)
  between operations  0.64 us (2%)
    pallas_call x1, Pallas kernels, per_device(): pl.pallas_call(functools.partial(kernel, n_z, shard, p_dev, wedges, units...  29.6 us
    pallas_call x1, Pallas kernels, per_device(): pl.pallas_call(finish, out_shape=(jax.ShapeDtypeStruct((CLASSES_PER_GROUP...  1.8 us

profile of v2, /device:TPU:0, one launch (start us, length us, event | category | flops | bytes accessed | tf_op | source)
XLA Modules:
  0.0 32.0 jit_solution(4492270898317331289)
XLA Ops:
  0.6 29.6 %shard_map.59 = (f32[4,13824]{1,0:T(4,128)}, f32[4,13824]{1,0:T(4,128)}) custom-call(s32[8]{0:T(128)} %bitcast.1, s32[8]{0:T(128)} %wedge_ref.1, bf16[8,2,110592]{2,1,0:T(2,128)(2,1)} %x_ref.1, f32[12,110592]{1,0:T(8,128)} %table_ref.1), custom_call_target="tpu_custom_call" | custom-call | tf_op jit(solution)/shard_map/pallas_call | solution.py:453
  30.2 1.8 %shard_map.60 = (f32[2,2,13824]{2,1,0:T(2,128)}, f32[2,13824]{1,0:T(2,128)}) custom-call(f32[4,13824]{1,0:T(4,128)} %get-tuple-element.4.mean_ref, f32[4,13824]{1,0:T(4,128)} %get-tuple-element.5.total_ref), custom_call_target="tpu_custom_call" | custom-call | tf_op jit(solution)/shard_map/pallas_call | solution.py:466

commit v3 on v2

--- a/solution.py
+++ b/solution.py
@@ -90,7 +90,7 @@
     label_s, wedge_s, aux_own, aux_peer, x_all, table, weights, sums, inverse, tops, tallies,
     q1, r1, q2, r2, q3, r3, t3, u3,
     small_sem, load_sem, table_sem, pair_send, pair_recv, aux_send, aux_recv,
-    s1, g1, s2, g2, s3, g3, ts, tg, ready,
+    s1, g1, s2, g2, s3, g3, ts, tg, ready, up, down,
 ):
     cls = lax.axis_index("cls")
     dom = lax.axis_index("dom")
@@ -150,8 +150,15 @@
         pl.semaphore_wait(ready, 1)
         signal(barrier, {"cls": near})
         signal(barrier, {"cls": far})
-        for step in range(last):
-            signal(barrier, {"dom": place(step) * 2 + core})
+
+        @pl.when(z > 0)
+        def _():
+            signal(barrier, {"dom": dom - 2})
+
+        @pl.when(z < last)
+        def _():
+            signal(barrier, {"dom": dom + 2})
+
 
     for copy in small:
         copy.wait()
@@ -283,7 +290,43 @@
     def all_entered():
         @pl.when(core == 1)
         def _():
-            pl.semaphore_wait(barrier, n_z + 1)
+            pl.semaphore_wait(barrier, 2 + jnp.minimum(z, 1) + jnp.minimum(last - z, 1))
+            signal(ready, {"dom": peer})
+
+        @pl.when(core == 0)
+        def _():
+            pl.semaphore_wait(ready, 1)
+
+    def tell(gap):
+        @pl.when((core == 1) & (z > 0) & (z + gap - 1 <= last))
+        def _():
+            signal(up.at[gap], {"dom": dom - 2})
+
+        @pl.when((core == 1) & (z < last) & (z - gap + 1 >= 0))
+        def _():
+            signal(down.at[gap], {"dom": dom + 2})
+
+    def hear(gap):
+        @pl.when((core == 1) & (z + gap <= last))
+        def _():
+            pl.semaphore_wait(up.at[gap], 1)
+
+        @pl.when((core == 1) & (z - gap >= 0))
+        def _():
+            pl.semaphore_wait(down.at[gap], 1)
+
+    rounds = [functools.partial(tell, 2)] if last >= 2 else []
+    for gap in range(2, last + 1):
+        rounds.append(functools.partial(hear, gap))
+        if gap < last:
+            rounds.append(functools.partial(tell, gap + 1))
+
+    def column_entered():
+        while rounds:
+            rounds.pop(0)()
+
+        @pl.when(core == 1)
+        def _():
             signal(ready, {"dom": peer})
 
         @pl.when(core == 0)
@@ -322,6 +365,7 @@
         step, part, start, count, kind = units[index]
         second[index].wait()
         if index == 0:
+            column_entered()
             t3[...] = tallies[pl.ds(0, GROUP_ROWS)] + from_code(r2[step, :, head(index, 1)])
             for other in range(last):
                 tally_copies.append(
@@ -388,6 +432,8 @@
     pick_weights(0)
     for turn in range(n_units):
         compute(turn)
+        for _ in range(min(len(rounds), 2 if turn else 1)):
+            rounds.pop(0)()
         if turn + 1 < n_units and units[turn + 1][0] > units[turn][0]:
             pick_weights(units[turn + 1][0])
         if turn == 7:
@@ -410,10 +456,21 @@
         settle(k)
 
 
-def finish(mean_ref, total_ref, avg_out, total_out):
+def finish(mean_ref, total_ref, avg_out, total_out, sem):
+    copies = []
     for index in range(avg_out.shape[0]):
-        avg_out[index] = mean_ref[pl.ds(2 * index, 2)]
-        total_out[pl.ds(index, 1)] = total_ref[pl.ds(2 * index, 1)]
+        copies.append(
+            pltpu.make_async_copy(mean_ref.at[pl.ds(2 * index, 2)], avg_out.at[index], sem.at[2 * index])
+        )
+        copies.append(
+            pltpu.make_async_copy(
+                total_ref.at[pl.ds(2 * index, 1)], total_out.at[pl.ds(index, 1)], sem.at[2 * index + 1]
+            )
+        )
+    for copy in copies:
+        copy.start()
+    for copy in copies:
+        copy.wait()
 
 
 def per_device(particles, labels, wedge_index, wedge_table):
@@ -450,11 +507,12 @@
     scratch += [dma((2,)), dma((n_z, p_dev)), dma((n_z,)), dma((n_z, p_dev)), dma((n_z, p_dev)), dma, dma]
     scratch += [dma((count,))] * 6
     scratch += [dma((n_z,))] * 2 + [pltpu.SemaphoreType.REGULAR]
+    scratch += [pltpu.SemaphoreType.REGULAR((n_z,))] * 2
     mean, total = pl.pallas_call(
         functools.partial(kernel, n_z, shard, p_dev, wedges, units),
         out_shape=(
-            jax.ShapeDtypeStruct((GROUP_ROWS, shard), f32),
-            jax.ShapeDtypeStruct((GROUP_ROWS, shard), f32),
+            pltpu.VMEM((GROUP_ROWS, shard), f32),
+            pltpu.VMEM((GROUP_ROWS, shard), f32),
         ),
         in_specs=[any_space] * 4,
         out_specs=(vmem, vmem),
@@ -469,8 +527,10 @@
             jax.ShapeDtypeStruct((CLASSES_PER_GROUP, 2, shard), f32),
             jax.ShapeDtypeStruct((CLASSES_PER_GROUP, shard), f32),
         ),
-        in_specs=[vmem, vmem],
-        out_specs=(vmem, vmem),
+        in_specs=[any_space, any_space],
+        out_specs=(any_space, any_space),
+        compiler_params=pltpu.CompilerParams(vmem_limit_bytes=4 * 1024 * 1024),
+        scratch_shapes=[dma((2 * CLASSES_PER_GROUP,))],
     )(mean, total)
 
 

time: 32.2 us -> 30.1 us (0.935)
  Pallas kernels: 31.4 us -> 29.3 us
    pallas_call x1, Pallas kernels: 1.8 us -> 0.75 us  [per_device(): pl.pallas_call(finish, out_shape=(jax.ShapeDtypeStruct((CLASSES_PER_GROUP...]
    pallas_call x1, Pallas kernels: 29.6 us -> 28.6 us  [per_device(): pl.pallas_call(functools.partial(kernel, n_z, shard, p_dev, wedges, units...]
where the time goes in v3:
time: 30.1 us; the launch traced here: 30 us
  Pallas kernels  29.3 us (97%)
  between operations  0.64 us (2%)
    pallas_call x1, Pallas kernels, per_device(): pl.pallas_call(functools.partial(kernel, n_z, shard, p_dev, wedges, units...  28.6 us
    pallas_call x1, Pallas kernels, per_device(): pl.pallas_call(finish, out_shape=(jax.ShapeDtypeStruct((CLASSES_PER_GROUP...  0.75 us

profile of v3, /device:TPU:0, one launch (start us, length us, event | category | flops | bytes accessed | tf_op | source)
XLA Modules:
  0.0 30.0 jit_solution(13021401599943445929)
XLA Ops:
  0.6 28.6 %shard_map.59 = (f32[4,13824]{1,0:T(4,128)S(1)}, f32[4,13824]{1,0:T(4,128)S(1)}) custom-call(s32[8]{0:T(128)} %bitcast.1, s32[8]{0:T(128)} %wedge_ref.1, bf16[8,2,110592]{2,1,0:T(2,128)(2,1)} %x_ref.1, f32[12,110592]{1,0:T(8,128)} %table_ref.1), custom_call_target="tpu_custom_call" | custom-call | tf_op jit(solution)/shard_map/pallas_call | solution.py:511
  29.2 0.8 %shard_map.60 = (f32[2,2,13824]{2,1,0:T(2,128)}, f32[2,13824]{1,0:T(2,128)}) custom-call(f32[4,13824]{1,0:T(4,128)S(1)} %get-tuple-element.4.mean_ref, f32[4,13824]{1,0:T(4,128)S(1)} %get-tuple-element.5.total_ref), custom_call_target="tpu_custom_call" | custom-call | tf_op jit(solution)/shard_map/pallas_call | solution.py:524

commit v4 on v3

--- a/solution.py
+++ b/solution.py
@@ -16,15 +16,28 @@
 CLASSES_PER_GROUP = 2
 GROUP_ROWS = 2 * CLASSES_PER_GROUP
 PAIR_ROWS = 2 * GROUP_ROWS
-PICK_TILES = 36
-SUM_TILES = 27
+PICK_TILES = 108
+SUM_TILES = 54
 CODE_TILES = 27
-FORWARD_LAG = 2
-SETTLE_LAG = 4
+AHEAD = 2
+SETTLE_AFTER = 1
+OWN_PAIRS = 2
+EARLY_SHARE = 0.45
 
 
 def divisor(number, cap):
     return max(size for size in range(1, cap + 1) if number % size == 0)
+
+
+def padded(count):
+    return -(-count // 16) * 16
+
+
+def filled(value):
+    extra = padded(value.shape[0]) - value.shape[0]
+    if extra == 0:
+        return value
+    return jnp.concatenate([value, jnp.zeros((extra, value.shape[1]), value.dtype)], axis=0)
 
 
 def dot(left, right):
@@ -35,11 +48,6 @@
     high = value.astype(jnp.bfloat16)
     low = (value - high.astype(jnp.float32)).astype(jnp.bfloat16)
     return jnp.concatenate([high, low], axis=0)
-
-
-def stack2_rows(value):
-    high = value.astype(jnp.bfloat16).astype(jnp.float32)
-    return jnp.concatenate([high, value - high], axis=0).astype(jnp.bfloat16)
 
 
 def walk(start, tiles, cap, body):
@@ -76,21 +84,74 @@
 
 def plan_units(n_z, tiles):
     half = tiles // 2
-    plain = ((0, half, 0), (half, tiles - half, 1))
-    units = []
+    early = int(tiles * EARLY_SHARE / 2)
+    units, pairs, firsts = [], [], []
+
+    def add(step, pieces, early=False):
+        base = sum(1 for unit in units if unit[0] == step)
+        names = []
+        for part, (start, count, kind) in enumerate(pieces):
+            names.append(len(units))
+            units.append((step, base + part, start * LANES, count, kind, early))
+        return names
+
     for step in range(n_z):
-        for part, (start, count, kind) in enumerate(plain):
-            units.append((step, part, start * LANES, count, kind))
-    return units
+        if step == n_z - 2 and early:
+            firsts = add(step, ((0, early, 0), (half, early, 1)), True)
+            pairs.append(add(step, ((early, half - early, 0), (half + early, tiles - half - early, 1))))
+        elif step == n_z - 1 and OWN_PAIRS == 2 and half >= 2:
+            cut = half // 2
+            pairs.append(add(step, ((0, cut, 0), (half, cut, 1))))
+            pairs.append(add(step, ((cut, half - cut, 0), (half + cut, tiles - half - cut, 1))))
+        else:
+            pairs.append(add(step, ((0, half, 0), (half, tiles - half, 1))))
+    starts = [sorted(unit[2] for unit in units if unit[0] == step) for step in range(n_z)]
+    units = [(unit[0], starts[unit[0]].index(unit[2]), *unit[2:]) for unit in units]
+    return units, pairs, firsts
+
+
+def plan_order(n_z, units, pairs, firsts):
+    order, count = [], len(pairs)
+    own = [k for k, unit in enumerate(units) if unit[0] == n_z - 1]
+    ready = set()
+
+    def weights(step):
+        if step not in ready:
+            ready.add(step)
+            order.append(("P", step))
+
+    def compute(j):
+        if j < count:
+            weights(units[pairs[j][0]][0])
+            order.extend(("C", k) for k in pairs[j])
+
+    compute(0)
+    if firsts:
+        weights(n_z - 2)
+        order.extend(("Z", k) for k in firsts)
+    for j in range(1, AHEAD):
+        compute(j)
+    for j in range(count):
+        order.extend(("F", k) for k in pairs[j])
+        compute(j + AHEAD)
+        if j >= SETTLE_AFTER:
+            order.extend(("S", k) for k in pairs[j - SETTLE_AFTER] if k not in own)
+    late = [k for pair in pairs[count - SETTLE_AFTER :] for k in pair]
+    remote = [k for k, unit in enumerate(units) if unit[0] < n_z - 1 and not unit[5]]
+    order.extend(("S", k) for k in late if k not in own)
+    order.append(("T", 0))
+    order.extend(("G", k) for k in remote)
+    order.extend(("S", k) for k in own)
+    return order
 
 
 def kernel(
-    n_z, shard, p_dev, wedges, units,
+    n_z, shard, p_dev, wedges, units, script,
     labels_ref, wedge_ref, x_ref, table_ref, mean_ref, total_ref,
     label_s, wedge_s, aux_own, aux_peer, x_all, table, weights, sums, inverse, tops, tallies,
-    q1, r1, q2, r2, q3, r3, t3, u3,
+    q0, r0, q1, r1, q2, r2, q3, r3, t3, u3,
     small_sem, load_sem, table_sem, pair_send, pair_recv, aux_send, aux_recv,
-    s1, g1, s2, g2, s3, g3, ts, tg, ready, up, down,
+    s0, g0, s1, g1, g2, g3, ts, tg, ready, up, down,
 ):
     cls = lax.axis_index("cls")
     dom = lax.axis_index("dom")
@@ -103,6 +164,7 @@
     rows = 2 * p_dev
     tiles = shard // LANES
     last = n_z - 1
+    slots = padded(wedges)
     offsets = sorted(range(1, n_z), key=lambda gap: -min(gap, n_z - gap)) + [0]
 
     def place(step):
@@ -124,21 +186,56 @@
     def _():
         signal(barrier, {"dom": peer})
 
-    loads, tables = [], []
-    for step in range(n_z):
+    loads, tables, pair = [], [], []
+
+    def chunks(step, where):
+        base = (place(step) * 2 + where) * shard
+        cut = tiles // 2 * LANES if step == 0 else 0
+        spans = [(0, cut), (cut, shard - cut)] if cut else [(0, shard)]
+        return [
+            (pl.ds(pl.multiple_of(base + begin, LANES), size), pl.ds(begin, size))
+            for begin, size in spans
+        ]
+
+    def load_step(step):
         here = place(step) * 2 + core
         span = pl.ds(pl.multiple_of(here * shard, LANES), shard)
-        copy = pltpu.make_async_copy(table_ref.at[:, span], table.at[step], table_sem.at[step])
+        copy = pltpu.make_async_copy(
+            table_ref.at[:, span], table.at[step], table_sem.at[step]
+        )
         copy.start()
         tables.append(copy)
-        copies = []
-        for p in range(p_dev):
-            copy = pltpu.make_async_copy(
-                x_ref.at[p, :, span], x_all.at[step, pl.ds(2 * p, 2)], load_sem.at[step, p]
-            )
-            copy.start()
-            copies.append(copy)
-        loads.append(copies)
+        waits = []
+        for part, (source, target) in enumerate(chunks(step, core)):
+            for p in range(p_dev):
+                pltpu.make_async_copy(
+                    x_ref.at[p, :, source], x_all.at[step, pl.ds(2 * p, 2), target],
+                    load_sem.at[step, part],
+                ).start()
+            block = x_all.at[step, pl.ds(0, rows), target]
+            waits.append(pltpu.make_async_copy(block, block, load_sem.at[step, part]))
+        loads.append(waits)
+
+    def pair_step(step):
+        waits = []
+        for part, (source, target) in enumerate(chunks(step, 1 - core)):
+            def pair_copy(source, target):
+                return pltpu.make_async_remote_copy(
+                    src_ref=source, dst_ref=target,
+                    send_sem=pair_send, recv_sem=pair_recv.at[step, part],
+                    device_id={"dom": peer}, device_id_type=MESH,
+                )
+
+            for p in range(p_dev):
+                pair_copy(
+                    x_ref.at[p, :, source], x_all.at[step, pl.ds(rows + 2 * p, 2), target]
+                ).start()
+            block = x_all.at[step, pl.ds(rows, rows), target]
+            waits.append(pair_copy(block, block))
+        pair.append(waits)
+
+    for step in range(n_z):
+        load_step(step)
 
     @pl.when(core == 0)
     def _():
@@ -172,8 +269,8 @@
     for p in range(p_dev):
         wedge_of = jnp.where(row // 2 == p, wedge_s[p], wedge_of)
         label_of = jnp.where(particle == p, label_s[p], label_of)
-    column = jnp.where(lane >= wedges, lane - wedges, lane)
-    aux_own[0] = ((wedge_of == column) & (lane < 2 * wedges)).astype(jnp.float32)
+    column = jnp.where(lane >= slots, lane - slots, lane)
+    aux_own[0] = ((wedge_of == column) & (lane < 2 * slots)).astype(jnp.float32)
     within = (out_row // 2) % CLASSES_PER_GROUP
     place_of = out_row // GROUP_ROWS
     for kind, order in enumerate(((cls, far, near, both), (cls, near, far, both))):
@@ -189,20 +286,8 @@
         device_id={"dom": peer}, device_id_type=MESH,
     )
     aux_copy.start()
-    pair = []
     for step in range(n_z):
-        there = place(step) * 2 + (1 - core)
-        span = pl.ds(pl.multiple_of(there * shard, LANES), shard)
-        copies = []
-        for p in range(p_dev):
-            copy = pltpu.make_async_remote_copy(
-                src_ref=x_ref.at[p, :, span], dst_ref=x_all.at[step, pl.ds(rows + 2 * p, 2)],
-                send_sem=pair_send.at[step, p], recv_sem=pair_recv.at[step, p],
-                device_id={"dom": peer}, device_id_type=MESH,
-            )
-            copy.start()
-            copies.append(copy)
-        pair.append(copies)
+        pair_step(step)
     aux_copy.wait()
 
     own_side = (out_lane & rows) == 0
@@ -212,7 +297,7 @@
     ]
     pick = jnp.concatenate([aux_own[0], aux_peer[0]], axis=0).astype(jnp.bfloat16)
     counts = dot(members[0][:, : 2 * rows], pick)
-    pick = pick[:, : 2 * wedges]
+    pick = pick[:, : 2 * slots]
 
     def send(source, target, sems, who):
         copy = pltpu.make_async_remote_copy(
@@ -226,47 +311,112 @@
         tables[step].wait()
 
         def body(span, unit):
-            weights[step, :, span] = dot(pick, stack2_rows(table[step, :, span]))
+            weights[step, :, span] = dot(pick, stack2(filled(table[step, :, span])))
 
         walk(0, tiles, PICK_TILES, body)
 
     def wire(ref, index, tally=False):
-        step, part, start, count, kind = units[index]
+        step, part, start, count, kind, _ = units[index]
         begin = start + part * (HEAD * LANES)
         return ref.at[step, :, pl.ds(begin, (count + 1 + tally) * LANES)]
 
     def head(index, extra=0):
-        step, part, start, count, kind = units[index]
+        step, part, start, count, kind, _ = units[index]
         return pl.ds(start + part * (HEAD * LANES) + (count + extra) * LANES, LANES)
 
     def shifted(span, index):
         begin = span.start + units[index][1] * (HEAD * LANES)
         return pl.ds(begin if isinstance(begin, int) else pl.multiple_of(begin, LANES), span.size)
 
-    first, second, third, tally_copies = {}, {}, {}, []
+    zeroth, first, second, third, tally_copies = {}, {}, {}, {}, []
+    column_known = []
+
+    def pieces_of(index):
+        step, part, start, count, kind, _ = units[index]
+        if step != last:
+            return [(start, count, None)]
+        pieces, at, end = [], start, start + count * LANES
+        for k, unit in enumerate(units):
+            low, high = max(at, unit[2]), min(end, unit[2] + unit[3] * LANES)
+            if unit[5] and low < high:
+                if low > at:
+                    pieces.append((at, (low - at) // LANES, None))
+                pieces.append((low, (high - low) // LANES, k))
+                at = high
+        if at < end:
+            pieces.append((at, (end - at) // LANES, None))
+        return pieces
+
+    def number(index):
+        return index - len([k for k in range(index) if units[k][5]])
+
+    def early_slot(index):
+        slot = [k for k, unit in enumerate(units) if unit[5]].index(index)
+        return slot, (units[index][3] + 1) * LANES
+
+    def early_wire(ref, index):
+        slot, size = early_slot(index)
+        return ref.at[slot, :, pl.ds(0, size)]
+
+    loaded, landed = set(), set()
 
     def compute(index):
-        step, part, start, count, kind = units[index]
-        if start == 0:
-            for copy in loads[step] + pair[step]:
-                copy.wait()
+        step, part, start, count, kind, early = units[index]
+        groups = len(loads[step])
+        for group in range(1 if groups > 1 and start + count * LANES <= tiles // 2 * LANES else groups):
+            if (step, group) not in loaded:
+                loaded.add((step, group))
+                loads[step][group].wait()
+                pair[step][group].wait_recv()
         member = members[kind]
         tops[index] = jnp.zeros((4 * GROUP_ROWS, LANES), jnp.float32)
-
-        def body(span, unit):
-            product = weights[step, :, span] * x_all[step, :, span].astype(jnp.float32)
-            total = dot(member, stack2(product))
-            sums[step, :, span] = total
-            size = jnp.abs(total)
-            pieces = [size[:, k * LANES : (k + 1) * LANES] for k in range(unit)]
-            while len(pieces) > 1:
-                pieces = [
-                    jnp.maximum(*pieces[k : k + 2]) if k + 1 < len(pieces) else pieces[k]
-                    for k in range(0, len(pieces), 2)
-                ]
-            tops[index] = jnp.maximum(tops[index], pieces[0])
-
-        walk(start, count, SUM_TILES, body)
+        for begin, length, source in pieces_of(index):
+            scale = None
+            if source is not None:
+                slot = early_slot(source)[0]
+                if source not in landed:
+                    landed.add(source)
+                    zeroth[source].wait()
+                origin = units[source][2]
+                scale = scale_of(r0[slot, :, pl.ds(units[source][3] * LANES, LANES)]) * (1.0 / LEVELS)
+
+            def body(span, unit):
+                product = weights[step, :, span] * x_all[step, :, span].astype(jnp.float32)
+                total = dot(member, stack2(product))
+                if scale is not None:
+                    at = span.start - origin
+                    there = pl.ds(at if isinstance(at, int) else pl.multiple_of(at, LANES), span.size)
+                    total = total + from_code(r0[slot, :, there]) * wide(scale, unit)
+                sums[step, :, span] = total
+                size = jnp.abs(total)
+                parts = [size[:, k * LANES : (k + 1) * LANES] for k in range(unit)]
+                while len(parts) > 1:
+                    parts = [
+                        jnp.maximum(*parts[k : k + 2]) if k + 1 < len(parts) else parts[k]
+                        for k in range(0, len(parts), 2)
+                    ]
+                tops[index] = jnp.maximum(tops[index], parts[0])
+
+            walk(begin, length, SUM_TILES, body)
+        span = pl.ds(start, count * LANES)
+        if early:
+            slot, size = early_slot(index)
+            code = scale_code(jnp.maximum(tops[index], TINY))
+            q0[slot, :, pl.ds(count * LANES, LANES)] = code
+            factor = LEVELS / scale_of(code)
+
+            def early_body(span, unit):
+                at = span.start - start
+                there = pl.ds(at if isinstance(at, int) else pl.multiple_of(at, LANES), span.size)
+                q0[slot, :, there] = to_code(sums[step, :, span] * wide(factor, unit))
+
+            walk(start, count, CODE_TILES, early_body)
+            column_entered()
+            zeroth[index] = send(
+                early_wire(q0, index), early_wire(r0, index), (s0.at[slot], g0.at[slot]),
+                {"dom": place(step) * 2 + core},
+            )
+            return
         code = scale_code(jnp.maximum(tops[index, pl.ds(PAIR_ROWS, PAIR_ROWS)], TINY))
         q1[step, :, head(index)] = code
         if index == 0:
@@ -284,7 +434,7 @@
         partner = near if kind == 0 else far
         first[index] = send(
             wire(q1, index, index == 0), wire(r1, index, index == 0),
-            (s1.at[index], g1.at[index]), {"cls": partner},
+            (s1.at[number(index)], g1.at[number(index)]), {"cls": partner},
         )
 
     def all_entered():
@@ -300,20 +450,20 @@
     def tell(gap):
         @pl.when((core == 1) & (z > 0) & (z + gap - 1 <= last))
         def _():
-            signal(up.at[gap], {"dom": dom - 2})
+            signal(up.at[gap - 2], {"dom": dom - 2})
 
         @pl.when((core == 1) & (z < last) & (z - gap + 1 >= 0))
         def _():
-            signal(down.at[gap], {"dom": dom + 2})
+            signal(down.at[gap - 2], {"dom": dom + 2})
 
     def hear(gap):
         @pl.when((core == 1) & (z + gap <= last))
         def _():
-            pl.semaphore_wait(up.at[gap], 1)
+            pl.semaphore_wait(up.at[gap - 2], 1)
 
         @pl.when((core == 1) & (z - gap >= 0))
         def _():
-            pl.semaphore_wait(down.at[gap], 1)
+            pl.semaphore_wait(down.at[gap - 2], 1)
 
     rounds = [functools.partial(tell, 2)] if last >= 2 else []
     for gap in range(2, last + 1):
@@ -322,6 +472,9 @@
             rounds.append(functools.partial(tell, gap + 1))
 
     def column_entered():
+        if column_known:
+            return
+        column_known.append(True)
         while rounds:
             rounds.pop(0)()
 
@@ -334,7 +487,7 @@
             pl.semaphore_wait(ready, 1)
 
     def forward(index):
-        step, part, start, count, kind = units[index]
+        step, part, start, count, kind, _ = units[index]
         first[index].wait()
         got = scale_of(r1[step, :, head(index)])
         code = scale_code(jnp.maximum(tops[index, pl.ds(0, PAIR_ROWS)], TINY) + got)
@@ -358,11 +511,11 @@
         other = far if kind == 0 else near
         second[index] = send(
             wire(q2, index, index == 0), wire(r2, index, index == 0),
-            (s2.at[index], g2.at[index]), {"cls": other},
+            (s1.at[number(index)], g2.at[number(index)]), {"cls": other},
         )
 
     def settle(index):
-        step, part, start, count, kind = units[index]
+        step, part, start, count, kind, _ = units[index]
         second[index].wait()
         if index == 0:
             column_entered()
@@ -393,22 +546,19 @@
 
         walk(start, count, CODE_TILES, body)
         third[index] = send(
-            wire(q3, index), wire(r3, index), (s3.at[index], g3.at[index]),
+            wire(q3, index), wire(r3, index), (s1.at[number(index)], g3.at[number(index)]),
             {"dom": place(step) * 2 + core},
         )
 
     def gather(index):
-        step, part, start, count, kind = units[index]
-        mine = [k for k, unit in enumerate(units) if unit[0] < last and unit[1] == part]
-        for k in mine:
-            third[k].wait()
-        scales = [scale_of(r3[units[k][0], :, head(k)]) * (1.0 / LEVELS) for k in mine]
+        step, part, start, count, kind, _ = units[index]
+        third[index].wait()
+        scale = scale_of(r3[step, :, head(index)]) * (1.0 / LEVELS)
 
         def body(span, unit):
-            value = sums[step, pl.ds(0, GROUP_ROWS), span]
-            for k, scale in zip(mine, scales):
-                value = value + from_code(r3[units[k][0], :, shifted(span, k)]) * wide(scale, unit)
-            sums[step, pl.ds(0, GROUP_ROWS), span] = value
+            sums[last, pl.ds(0, GROUP_ROWS), span] = sums[last, pl.ds(0, GROUP_ROWS), span] + from_code(
+                r3[step, :, shifted(span, index)]
+            ) * wide(scale, unit)
 
         walk(start, count, CODE_TILES, body)
 
@@ -417,43 +567,35 @@
         for step in range(last):
             tally_copies[step].wait()
             tally = tally + u3[step]
-        tally = stack2_rows(tally[:, : 2 * wedges])
+        high = tally.astype(jnp.bfloat16).astype(jnp.float32)
+        tally = jnp.concatenate([high, tally - high], axis=0)[:, : 2 * slots].astype(jnp.bfloat16)
 
         def body(span, unit):
-            weight = table[last, :, span]
-            total = dot(tally, stack2_rows(weight * weight))
+            weight = filled(table[last, :, span])
+            total = dot(tally, stack2(weight * weight))
             total = total[:GROUP_ROWS] + total[GROUP_ROWS:]
             total_ref[:, span] = total
             inverse[:, span] = 1.0 / (total + 1.0)
 
         walk(0, tiles, SUM_TILES, body)
 
-    n_units = len(units)
-    pick_weights(0)
-    for turn in range(n_units):
-        compute(turn)
-        for _ in range(min(len(rounds), 2 if turn else 1)):
-            rounds.pop(0)()
-        if turn + 1 < n_units and units[turn + 1][0] > units[turn][0]:
-            pick_weights(units[turn + 1][0])
-        if turn == 7:
+    for name, index in script:
+        if name == "P":
+            pick_weights(index)
+        elif name in "CZ":
+            compute(index)
+            for _ in range(min(len(rounds), 2 if index else 1)):
+                rounds.pop(0)()
+        elif name == "F":
+            forward(index)
+        elif name == "S":
+            settle(index)
+        elif name == "G":
+            gather(index)
+        else:
             tally_final()
-        if turn >= FORWARD_LAG:
-            forward(turn - FORWARD_LAG)
-        if turn >= SETTLE_LAG:
-            settle(turn - SETTLE_LAG)
-    lasts = [k for k, unit in enumerate(units) if unit[0] == last]
-    pending = [k for k in range(max(0, n_units - SETTLE_LAG), n_units)]
-    for k in range(max(0, n_units - FORWARD_LAG), n_units):
-        forward(k)
-        if pending and pending[0] not in lasts:
-            settle(pending.pop(0))
-    while pending and pending[0] not in lasts:
-        settle(pending.pop(0))
-    for k in lasts:
-        gather(k)
-    for k in pending:
-        settle(k)
+            sent = x_all.at[:, pl.ds(rows, rows)]
+            pltpu.make_async_copy(sent, sent, pair_send).wait()
 
 
 def finish(mean_ref, total_ref, avg_out, total_out, sem):
@@ -481,8 +623,11 @@
     n_z = n_dom // 2
     rows = 2 * p_dev
     tiles = shard // LANES
-    units = plan_units(n_z, tiles)
+    units, pairs, firsts = plan_units(n_z, tiles)
+    order = plan_order(n_z, units, pairs, firsts)
     count = len(units)
+    widest = max([units[k][3] for k in firsts], default=0) + 1
+    parts = max(unit[1] for unit in units) + 1
     any_space = pl.BlockSpec(memory_space=pl.ANY)
     vmem = pl.BlockSpec(memory_space=pltpu.VMEM)
     dma = pltpu.SemaphoreType.DMA
@@ -500,16 +645,18 @@
         pltpu.VMEM((count, 4 * GROUP_ROWS, LANES), f32),
         pltpu.VMEM((PAIR_ROWS, LANES), f32),
     ]
-    long = shard + len([unit for unit in units if unit[0] == 0]) * HEAD * LANES
+    long = shard + parts * HEAD * LANES
+    scratch += [pltpu.VMEM((max(len(firsts), 1), 4 * GROUP_ROWS, widest * LANES), jnp.int16)] * 2
     for height in (PAIR_ROWS, GROUP_ROWS, GROUP_ROWS):
         scratch += [pltpu.VMEM((n_z, height, long), jnp.int16)] * 2
     scratch += [pltpu.VMEM((GROUP_ROWS, LANES), f32), pltpu.VMEM((n_z, GROUP_ROWS, LANES), f32)]
-    scratch += [dma((2,)), dma((n_z, p_dev)), dma((n_z,)), dma((n_z, p_dev)), dma((n_z, p_dev)), dma, dma]
-    scratch += [dma((count,))] * 6
-    scratch += [dma((n_z,))] * 2 + [pltpu.SemaphoreType.REGULAR]
-    scratch += [pltpu.SemaphoreType.REGULAR((n_z,))] * 2
+    scratch += [dma((2,)), dma((n_z, 2)), dma((n_z,)), dma, dma((n_z, 2)), dma, dma]
+    remote = len([unit for unit in units if unit[0] < n_z - 1 and not unit[5]])
+    scratch += [dma((max(len(firsts), 1),))] * 2 + [dma((count - len(firsts),))] * 3 + [dma((remote,))]
+    scratch += [dma((n_z - 1,))] * 2 + [pltpu.SemaphoreType.REGULAR]
+    scratch += [pltpu.SemaphoreType.REGULAR((max(n_z - 2, 1),))] * 2
     mean, total = pl.pallas_call(
-        functools.partial(kernel, n_z, shard, p_dev, wedges, units),
+        functools.partial(kernel, n_z, shard, p_dev, wedges, units, order),
         out_shape=(
             pltpu.VMEM((GROUP_ROWS, shard), f32),
             pltpu.VMEM((GROUP_ROWS, shard), f32),

time: 30.1 us -> 26.6 us (0.88)
  Pallas kernels: 29.3 us -> 25.8 us
    pallas_call x1, Pallas kernels: 28.6 us -> 25 us  [per_device(): pl.pallas_call(functools.partial(kernel, n_z, shard, p_dev, wedges, units...]
where the time goes in v4:
time: 26.6 us; the launch traced here: 26.4 us
  Pallas kernels  25.8 us (97%)
  between operations  0.64 us (2%)
    pallas_call x1, Pallas kernels, per_device(): pl.pallas_call(functools.partial(kernel, n_z, shard, p_dev, wedges, units...  25 us
    pallas_call x1, Pallas kernels, per_device(): pl.pallas_call(finish, out_shape=(jax.ShapeDtypeStruct((CLASSES_PER_GROUP...  0.75 us

profile of v4, /device:TPU:0, one launch (start us, length us, event | category | flops | bytes accessed | tf_op | source)
XLA Modules:
  0.0 26.4 jit_solution(2718668447382317024)
XLA Ops:
  0.6 25.0 %shard_map.59 = (f32[4,13824]{1,0:T(4,128)S(1)}, f32[4,13824]{1,0:T(4,128)S(1)}) custom-call(s32[8]{0:T(128)} %bitcast.1, s32[8]{0:T(128)} %wedge_ref.1, bf16[8,2,110592]{2,1,0:T(2,128)(2,1)} %x_ref.1, f32[12,110592]{1,0:T(8,128)} %table_ref.1), custom_call_target="tpu_custom_call" | custom-call | tf_op jit(solution)/shard_map/pallas_call | solution.py:658
  25.7 0.8 %shard_map.60 = (f32[2,2,13824]{2,1,0:T(2,128)}, f32[2,13824]{1,0:T(2,128)}) custom-call(f32[4,13824]{1,0:T(4,128)S(1)} %get-tuple-element.4.mean_ref, f32[4,13824]{1,0:T(4,128)S(1)} %get-tuple-element.5.total_ref), custom_call_target="tpu_custom_call" | custom-call | tf_op jit(solution)/shard_map/pallas_call | solution.py:671

commit v5 on v4

--- a/solution.py
+++ b/solution.py
@@ -18,7 +18,7 @@
 PAIR_ROWS = 2 * GROUP_ROWS
 PICK_TILES = 108
 SUM_TILES = 54
-CODE_TILES = 27
+CODE_TILES = 54
 AHEAD = 2
 SETTLE_AFTER = 1
 OWN_PAIRS = 2
@@ -131,15 +131,16 @@
         order.extend(("Z", k) for k in firsts)
     for j in range(1, AHEAD):
         compute(j)
+    remote = [k for k, unit in enumerate(units) if unit[0] < n_z - 1 and not unit[5]]
     for j in range(count):
+        if j == count - 1:
+            order.append(("T", 0))
         order.extend(("F", k) for k in pairs[j])
         compute(j + AHEAD)
         if j >= SETTLE_AFTER:
             order.extend(("S", k) for k in pairs[j - SETTLE_AFTER] if k not in own)
     late = [k for pair in pairs[count - SETTLE_AFTER :] for k in pair]
-    remote = [k for k, unit in enumerate(units) if unit[0] < n_z - 1 and not unit[5]]
     order.extend(("S", k) for k in late if k not in own)
-    order.append(("T", 0))
     order.extend(("G", k) for k in remote)
     order.extend(("S", k) for k in own)
     return order

time: 26.6 us -> 26.5 us (level)
  no operation moved by 1% of the time
where the time goes in v5:
time: 26.5 us; the launch traced here: 26.4 us
  Pallas kernels  25.7 us (97%)
  between operations  0.64 us (2%)
    pallas_call x1, Pallas kernels, per_device(): pl.pallas_call(functools.partial(kernel, n_z, shard, p_dev, wedges, units...  25 us
    pallas_call x1, Pallas kernels, per_device(): pl.pallas_call(finish, out_shape=(jax.ShapeDtypeStruct((CLASSES_PER_GROUP...  0.75 us

profile of v5, /device:TPU:0, one launch (start us, length us, event | category | flops | bytes accessed | tf_op | source)
XLA Modules:
  0.0 26.4 jit_solution(11636952155700518189)
XLA Ops:
  0.6 25.0 %shard_map.59 = (f32[4,13824]{1,0:T(4,128)S(1)}, f32[4,13824]{1,0:T(4,128)S(1)}) custom-call(s32[8]{0:T(128)} %bitcast.1, s32[8]{0:T(128)} %wedge_ref.1, bf16[8,2,110592]{2,1,0:T(2,128)(2,1)} %x_ref.1, f32[12,110592]{1,0:T(8,128)} %table_ref.1), custom_call_target="tpu_custom_call" | custom-call | tf_op jit(solution)/shard_map/pallas_call | solution.py:659
  25.6 0.8 %shard_map.60 = (f32[2,2,13824]{2,1,0:T(2,128)}, f32[2,13824]{1,0:T(2,128)}) custom-call(f32[4,13824]{1,0:T(4,128)S(1)} %get-tuple-element.4.mean_ref, f32[4,13824]{1,0:T(4,128)S(1)} %get-tuple-element.5.total_ref), custom_call_target="tpu_custom_call" | custom-call | tf_op jit(solution)/shard_map/pallas_call | solution.py:672
